TPU v7x, 32 devices: a whole 2x2x4 slice. The times are simulated.
32 devices in a mesh: comp: 2 (over core), dom: 16 (over z, y, x).
Axes of the slice: x: 2, y: 2, z: 4, core: 2. Of those that a mesh axis runs over, the one named last changes fastest.
Arguments:
- surface_flux: float32 [6, 12, 131072], P(None, None, ('comp', 'dom')), may hold values from -8 to 8
- active_mask: int32 [131072], P(('comp', 'dom')), may hold values 0 or 1
- source_area: float32 [131072], P(('comp', 'dom')), may hold values from 0.5 to 30
- tile_targets: int32 [2048, 2], P(('comp', 'dom')), may hold values from 0 to 31, all different within a row
- remap_tiles: float32 [2048, 2, 64, 384], P(('comp', 'dom')), may hold values from -0.0625 to 0.0625
- ocean_flux: float32 [12, 12288], P(None, ('comp', 'dom')), may hold values from -6 to 6
- air_fraction: float32 [3, 12288], P(None, ('comp', 'dom')), may hold values from 0 to 1, as said below
- air_area: float32 [12288], P(('comp', 'dom')), may hold values from 0.5 to 30
Outputs:
- merged: float32 [12, 12288], P(None, ('comp', 'dom'))
- area_means: float32 [3, 12], replicated
Inputs may be any that keep to these rules, and one draw needn't show every extreme that they name: `air_fraction`: the three fractions of a cell are positive and sum to one. `tile_targets`: the 2 targets of one source block differ.
All inputs are finite; a program needn't handle non-finite values. No bound on the sum of `active_mask` on one device may be relied on, other than what follows from the above.
Results may differ from a plain program's by a relative error of at most 0.000071.
Values sent between devices are 32-bit elements; how exact they have to be, the bound alone decides.
A program may use at most 64 MiB of HBM per device.

v0:
```python
import jax
import jax.numpy as jnp
from jax import lax
from jax.sharding import PartitionSpec as P


def on_device(
    surface_flux,
    active_mask,
    source_area,
    tile_targets,
    remap_tiles,
    ocean_flux,
    air_fraction,
    air_area,
):
    step_count = surface_flux.shape[0]
    field_count = surface_flux.shape[1]
    block_count, intersection, block_cells, air_cells = remap_tiles.shape
    group_count = lax.axis_size("comp")
    domain_count = lax.axis_size("dom")
    owner_count = group_count * domain_count
    coverage = active_mask.astype(jnp.float32) * source_area
    average = jnp.sum(surface_flux, axis=0) / step_count
    weighted = average * coverage[None, :]
    blocks = weighted.reshape(field_count, block_count, block_cells)
    contrib = jnp.einsum("fbs,btsa->btfa", blocks, remap_tiles, precision=lax.Precision.HIGHEST)
    contrib = contrib.reshape(block_count * intersection, field_count * air_cells)
    targets = tile_targets.reshape(block_count * intersection)
    own_group = lax.axis_index("comp")
    group_pick = (jnp.arange(group_count, dtype=jnp.int32) == own_group).astype(jnp.float32)
    surface_num = group_pick[:, None] * jnp.sum(weighted, axis=1)[None, :]
    surface_den = group_pick * jnp.sum(source_area)
    owner_ids = jnp.arange(owner_count, dtype=jnp.int32)
    selector = (targets[None, :] == owner_ids[:, None]).astype(jnp.float32)
    outgoing = jnp.dot(selector, contrib, precision=lax.Precision.HIGHEST)
    incoming = lax.all_to_all(outgoing, ("comp", "dom"), split_axis=0, concat_axis=0, tiled=True)
    owner_sums = jnp.sum(
        incoming.reshape(group_count, domain_count, field_count * air_cells), axis=1
    )
    remapped = owner_sums.reshape(group_count, field_count, air_cells) / air_area[None, None, :]
    merged = (
        air_fraction[0][None, :] * remapped[0]
        + air_fraction[1][None, :] * remapped[1]
        + air_fraction[2][None, :] * ocean_flux
    )
    air_num = jnp.sum(merged * air_area[None, :], axis=1)
    air_den = jnp.sum(air_area)
    joined = lax.psum(
        (
            jnp.concatenate([surface_num, air_num[None, :]], axis=0),
            jnp.concatenate([surface_den, air_den[None]], axis=0),
        ),
        ("comp", "dom"),
    )
    numerators = joined[0]
    denominators = joined[1]
    area_means = numerators / denominators[:, None]
    return (merged, area_means)


def solution(mesh):
    in_specs = (
        P(None, None, ("comp", "dom")),
        P(("comp", "dom")),
        P(("comp", "dom")),
        P(("comp", "dom"), None),
        P(("comp", "dom"), None, None, None),
        P(None, ("comp", "dom")),
        P(None, ("comp", "dom")),
        P(("comp", "dom")),
    )
    out_specs = (P(None, ("comp", "dom")), P())
    return jax.shard_map(
        on_device, mesh=mesh, in_specs=in_specs, out_specs=out_specs, check_vma=False
    )
```

profile of v0, /device:TPU:10, one launch (start us, length us, event | category | flops | bytes accessed | tf_op | source)
XLA Modules:
  0.0 81.6 jit_solution(15840653103286598785)
XLA Ops:
  0.6 1.3 %fusion.8 = (f32[]{:T(128)}, f32[4096]{0:T(1024)S(1)}) fusion(f32[4096]{0:T(1024)} %param.10, s32[4096]{0:T(1024)} %param.9), kind=kLoop, calls=%fused_computation.25 | loop fusion | flops 16383 | bytes 49156 | tf_op jit(solution)/shard_map/reduce_sum | solution.py:33
  2.0 0.1 mul.84
  2.0 0.8 copy.13
  2.8 0.1 eq.25
  3.0 1.5 %reduce_sum.56 = f32[12,4096]{1,0:T(8,128)S(1)} reduce(f32[6,12,4096]{2,1,0:T(8,128)} %param.8, f32[]{:T(128)} %constant.8.clone.1), dimensions={0}, to_apply=%region_0.0 | reduce | flops 245760 | bytes 1376260 | tf_op jit(solution)/shard_map/reduce_sum | solution.py:24
  4.5 0.2 reduce_sum.57
  4.7 9.2 %fusion = f32[64,12,2,384]{3,1,2,0:T(8,128)S(1)} fusion(f32[64,2,64,384]{3,2,1,0:T(8,128)} %param.12, f32[12,64,64,1]{2,1,0,3:T(8,128)S(1)} %multiply_bitcast_fusion), kind=kOutput, calls=%fused_computation.1 | convolution fusion | flops 452984832 | bytes 15138816 | tf_op jit(solution)/shard_map/fbs,btsa->btfa/dot_general | solution.py:27
  13.8 0.7 copy.20
  14.6 0.0 copy-start.1
  14.6 0.0 copy-start.2
  14.6 0.0 copy-start
  14.6 1.0 %convolution_bitcast_fusion = f32[32,1,4608]{2,0,1:T(8,128)S(1)} fusion(f32[128,4608]{1,0:T(8,128)S(1)} %bitcast.30, s32[128]{0:T(128)S(1)} %eq.25), kind=kOutput, calls=%fused_computation | convolution fusion | flops 226496512 | bytes 2949632 | tf_op jit(solution)/shard_map/dot_general | solution.py:36
  15.6 1.4 %copy.15 = f32[32,1,4608]{2,1,0:T(1,128)} copy(f32[32,1,4608]{2,0,1:T(8,128)S(1)} %convolution_bitcast_fusion) | data formatting | bytes 1179648 | tf_op jit(solution)/shard_map/all_to_all | solution.py:37
  17.0 6.0 %all-to-all-start = ((f32[32,1,4608]{2,1,0:T(1,128)}), f32[32,1,4608]{2,1,0:T(1,128)S(1)}, u32[]{:S(2)}, u32[]{:S(2)}) async-start(f32[32,1,4608]{2,1,0:T(1,128)} %copy.15), calls=%async_computation | async-start | bytes 1179648 | tf_op jit(solution)/shard_map/all_to_all | solution.py:37
  23.0 0.0 copy-done.1
  23.1 0.6 reduce_sum.62
  23.7 0.6 compare_select_fusion
  24.3 0.7 pad_maximum_fusion.1
  25.0 0.0 copy-done.2
  25.1 0.1 multiply_reduce_fusion
  25.2 0.1 broadcast_multiply_fusion
  25.3 13.5 %all-to-all-done = f32[32,1,4608]{2,1,0:T(1,128)S(1)} async-done(((f32[32,1,4608]{2,1,0:T(1,128)}), f32[32,1,4608]{2,1,0:T(1,128)S(1)}, u32[]{:S(2)}, u32[]{:S(2)}) %all-to-all-start) | async-done | bytes 589856 | tf_op jit(solution)/shard_map/all_to_all | solution.py:37
  38.8 0.1 reduce_sum.58
  39.0 0.0 copy-done
  39.0 0.7 multiply_reduce_fusion.1
  39.7 41.3 %all-reduce = (f32[3,12]{1,0:T(4,128)S(1)}, f32[3]{0:T(128)S(1)}) all-reduce(f32[3,12]{1,0:T(4,128)S(1)} %pad_maximum_fusion, f32[3]{0:T(128)S(1)} %pad_maximum_fusion.1), channel_id=1, replica_groups=mesh['comp'=2,'dom'=16] {'comp','dom'}, use_global_device_ids=true, to_apply=%region_4.0 | all-reduce | flops 39 | bytes 312 | tf_op jit(solution)/shard_map/psum | solution.py:49
  81.0 0.7 broadcast_divide_fusion.1
  (7 shorter events, 0.2 us)
Async XLA Ops:
  14.6 8.4 %copy-start.1 = (f32[384]{0:T(512)S(1)}, f32[384]{0:T(512)}, u32[]{:S(2)}) copy-start(f32[384]{0:T(512)} %param.15) | copy-start | bytes 4612
  14.6 10.4 %copy-start.2 = (f32[3,384]{1,0:T(4,128)S(1)}, f32[3,384]{1,0:T(4,128)}, u32[]{:S(2)}) copy-start(f32[3,384]{1,0:T(4,128)} %param.14) | copy-start | bytes 13828
  14.6 24.3 %copy-start = (f32[12,384]{1,0:T(8,128)S(1)}, f32[12,384]{1,0:T(8,128)}, u32[]{:S(2)}) copy-start(f32[12,384]{1,0:T(8,128)} %param.13) | copy-start | bytes 55300
  17.0 21.7 %all-to-all-start = ((f32[32,1,4608]{2,1,0:T(1,128)}), f32[32,1,4608]{2,1,0:T(1,128)S(1)}, u32[]{:S(2)}, u32[]{:S(2)}) async-start(f32[32,1,4608]{2,1,0:T(1,128)} %copy.15), calls=%async_computation | async-start | bytes 1179648 | tf_op jit(solution)/shard_map/all_to_all | solution.py:37
where the time goes:
time: 82.1 us; the launch traced here: 81.6 us
  blocking collectives  41.3 us (50%)
  waiting for transfers between devices  13.5 us (16%)
  matrix products  10.1 us (12%)
  other arithmetic  6.6 us (8%)
  starting transfers between devices  6.02 us (7%)
  local copies, waits for them, and re-layouts  3.41 us (4%)
    psum x1, blocking collectives, on_device(): lax.psum((jnp.concatenate([surface_num, air_num[None, :]], axis=0), jnp.c...  41.3 us
    all_to_all x1, waiting for transfers between devices, on_device(): lax.all_to_all(outgoing, ('comp', 'dom'), split_axis=0, concat_axis=0, ti...  13.5 us
    dot_general x1, matrix products, on_device(): jnp.einsum('fbs,btsa->btfa', blocks, remap_tiles, precision=lax.Precision...  9.16 us
    all_to_all x1, starting transfers between devices, on_device(): lax.all_to_all(outgoing, ('comp', 'dom'), split_axis=0, concat_axis=0, ti...  6.02 us
  transfers between devices with their start and end apart: 1, of which 1 were waited for; matrix products, arithmetic and copies ran while one was open for 3% of the time, Pallas kernels for 0%

commit v1 on v0

v1 whole, which is shorter than its diff:
```python
import functools

import jax
import jax.numpy as jnp
from jax import lax
from jax.experimental import pallas as pl
from jax.experimental.pallas import tpu as pltpu
from jax.sharding import PartitionSpec as P

MESH = pl.DeviceIdType.MESH
F32 = jnp.float32
BF16 = jnp.bfloat16
CHUNKS = 8


def split(x):
    hi = x.astype(BF16)
    lo = (x - hi.astype(F32)).astype(BF16)
    return hi, lo


def kernel(
    groups,
    domains,
    flux_hbm,
    mask_ref,
    area_ref,
    targets_ref,
    tiles_hbm,
    ocean_ref,
    fraction_ref,
    air_ref,
    merged_ref,
    means_ref,
    flux,
    tiles,
    weighted,
    contrib,
    picks,
    rows_out,
    rows_in,
    summed,
    partner_in,
    outgoing,
    incoming,
    air_rows,
    stat_out,
    stat_in,
    flux_sem,
    tile_sem,
    row_send,
    row_recv,
    stat_send,
    stat_recv,
    pair_send,
    pair_recv,
    main_send,
    main_recv,
):
    steps, fields, cells = flux.shape
    blocks, slots, block_cells, air_cells = tiles.shape
    owners = groups * domains
    per_chunk = blocks // CHUNKS
    lane_tiles = air_cells // 128
    tile_count = blocks * slots
    comp = lax.axis_index("comp")
    dom = lax.axis_index("dom")
    me = comp * domains + dom
    other = 1 - comp

    flux_copy = pltpu.make_async_copy(flux_hbm, flux, flux_sem)
    flux_copy.start()
    tile_copies = []
    for i in range(CHUNKS):
        part = pl.ds(i * per_chunk, per_chunk)
        copy = pltpu.make_async_copy(tiles_hbm.at[part], tiles.at[part], tile_sem.at[i])
        copy.start()
        tile_copies.append(copy)

    barrier = pltpu.get_barrier_semaphore()

    def device(p):
        return (p // domains, p % domains)

    @pl.loop(1, owners)
    def _(k):
        pl.semaphore_signal(
            barrier, inc=1, device_id=device((me + k) % owners), device_id_type=MESH
        )

    for c in range(groups):
        rows_out[c, :, pl.ds(0, air_cells)] = fraction_ref[pl.ds(c, 1), :]
        rows_out[c, :, pl.ds(air_cells, air_cells)] = air_ref[...]
    rows_in[me] = rows_out[comp]
    pl.semaphore_wait(barrier, owners - 1)

    def row_copy(k):
        p = (me + k) % owners
        return pltpu.make_async_remote_copy(
            src_ref=rows_out.at[p // domains],
            dst_ref=rows_in.at[me],
            send_sem=row_send.at[k],
            recv_sem=row_recv.at[me],
            device_id=device(p),
            device_id_type=MESH,
        )

    @pl.loop(1, owners)
    def _(k):
        row_copy(k).start()

    flux_copy.wait()
    weighted[pl.ds(8, 8), :] = jnp.zeros((8, cells), F32)
    width = 512

    def weigh(i, carry):
        total, area_total = carry
        part = pl.ds(pl.multiple_of(i * width, width), width)
        value = flux[0, :, part]
        for s in range(1, steps):
            value = value + flux[s, :, part]
        area = area_ref[:, part]
        value = (value / steps) * (mask_ref[:, part].astype(F32) * area)
        weighted[pl.ds(0, fields), part] = value
        return total + value, area_total + area

    total, area_total = lax.fori_loop(
        0,
        cells // width,
        weigh,
        (jnp.zeros((fields, width), F32), jnp.zeros((1, width), F32)),
    )
    surface_num = jnp.sum(total, axis=1, keepdims=True)
    surface_den = jnp.sum(area_total)

    lane = lax.broadcasted_iota(jnp.int32, (16, 128), 1)
    first = lane < block_cells
    blank = jnp.zeros((16, 128), BF16)

    def pair(j, carry):
        cell = pl.ds(pl.multiple_of(j * 128, 128), 128)
        w = weighted[:, cell]
        lhs = []
        for keep in (first, ~first):
            hi, lo = split(jnp.where(keep, w, 0.0))
            lhs.append(jnp.concatenate([hi, hi], axis=1))
            lhs.append(jnp.concatenate([lo, blank], axis=1))
        left = jnp.concatenate(lhs, axis=0)
        for t in range(slots):
            weights = tiles[pl.ds(2 * j, 2), t].reshape(2 * block_cells, air_cells)
            hi, lo = split(weights)
            right = jnp.concatenate([hi, lo], axis=0)
            r = jnp.dot(left, right, preferred_element_type=F32)
            even = r[0:16] + r[16:32]
            odd = r[32:48] + r[48:64]
            base = pl.multiple_of((t * blocks + 2 * j) * 16, 32)
            for q in range(lane_tiles):
                cut = slice(q * 128, (q + 1) * 128)
                contrib[q, pl.ds(base, 16), :] = even[:, cut]
                contrib[q, pl.ds(base + 16, 16), :] = odd[:, cut]
        return carry

    pairs = per_chunk // 2
    for i in range(CHUNKS):
        tile_copies[i].wait()
        lax.fori_loop(i * pairs, (i + 1) * pairs, pair, 0)

    picks[:, pl.ds(0, blocks)] = targets_ref[...]
    picks[:, pl.ds(blocks, blocks)] = targets_ref[...]
    picked = jnp.where(
        lax.broadcasted_iota(jnp.int32, (1, tile_count), 1) < blocks,
        picks[pl.ds(0, 1), :],
        picks[pl.ds(1, 1), :],
    )
    owner_ids = lax.broadcasted_iota(jnp.int32, (owners, tile_count), 0)
    selector = jnp.where(owner_ids == picked, 1.0, 0.0).astype(BF16)
    selector = jnp.concatenate([selector, selector], axis=1)

    @pl.loop(1, owners)
    def _(k):
        p = (me + k) % owners
        pltpu.make_async_remote_copy(
            src_ref=rows_out.at[0],
            dst_ref=rows_in.at[p],
            send_sem=row_send.at[k],
            recv_sem=row_recv.at[p],
            device_id=device(p),
            device_id_type=MESH,
        ).wait_recv()

    rows = rows_in[:, 0, :]
    fraction = rows[:, :air_cells]
    scale = fraction / rows[:, air_cells:]

    air_rows[...] = jnp.zeros(air_rows.shape, F32)

    def gather(f, carry):
        right = []
        for q in range(lane_tiles):
            hi, lo = split(contrib[q, pl.ds(f, tile_count, stride=16), :])
            right.append(jnp.concatenate([hi, lo], axis=0))
        s = jnp.dot(selector, jnp.concatenate(right, axis=1), preferred_element_type=F32)
        summed[f] = s * scale
        air_rows[pl.ds(f, 1), :] = jnp.sum(s * fraction, axis=0, keepdims=True)
        return carry

    lax.fori_loop(0, fields, gather, 0)

    pair_copy = pltpu.make_async_remote_copy(
        src_ref=summed.at[:, pl.ds(pl.multiple_of(other * domains, 8), domains), :],
        dst_ref=partner_in,
        send_sem=pair_send,
        recv_sem=pair_recv,
        device_id=(other, dom),
        device_id_type=MESH,
    )
    pair_copy.start()

    ocean = fraction_ref[pl.ds(2, 1), :] * ocean_ref[...]
    air_num = jnp.sum(air_rows[pl.ds(0, fields), :] + air_ref[...] * ocean, axis=1, keepdims=True)
    air_den = jnp.sum(air_ref[...])
    spot = lax.broadcasted_iota(jnp.int32, (fields, 128), 1)
    line = lax.broadcasted_iota(jnp.int32, (fields, 128), 0)
    stat = jnp.where(spot == line + 16 * comp, surface_num, 0.0)
    stat = stat + jnp.where(spot == line + 16 * groups, air_num, 0.0)
    stat = jnp.sum(stat, axis=0, keepdims=True)
    spot = lax.broadcasted_iota(jnp.int32, (1, 128), 1)
    dens = 16 * (groups + 1)
    stat = stat + jnp.where(spot == dens + comp, surface_den, 0.0)
    stat = stat + jnp.where(spot == dens + groups, air_den, 0.0)
    stat_out[...] = stat
    stat_in[me] = stat

    def stat_copy(k, slot):
        return pltpu.make_async_remote_copy(
            src_ref=stat_out,
            dst_ref=stat_in.at[slot],
            send_sem=stat_send.at[k],
            recv_sem=stat_recv.at[slot],
            device_id=device((me + k) % owners),
            device_id_type=MESH,
        )

    @pl.loop(1, owners)
    def _(k):
        stat_copy(k, me).start()

    pair_copy.wait()
    own = pl.ds(pl.multiple_of(comp * domains, 8), domains)
    for f in range(fields):
        outgoing[:, f, :] = summed[f, own, :] + partner_in[f]

    def main_copy(k, slot):
        p = (dom + k) % domains
        return pltpu.make_async_remote_copy(
            src_ref=outgoing.at[p],
            dst_ref=incoming.at[slot],
            send_sem=main_send.at[k],
            recv_sem=main_recv.at[slot],
            device_id=(comp, p),
            device_id_type=MESH,
        )

    @pl.loop(1, domains)
    def _(k):
        main_copy(k, dom).start()

    merged_ref[...] = ocean + outgoing[dom]

    @pl.loop(1, owners)
    def _(k):
        stat_copy(k, (me + k) % owners).wait_recv()

    stat = jnp.sum(stat_in[...], axis=0)
    for c in range(groups + 1):
        den = jnp.sum(jnp.where(spot == dens + c, stat, 0.0))
        moved = stat if c == 0 else pltpu.roll(stat, 128 - 16 * c, 1)
        means_ref[pl.ds(c, 1), :] = moved[:, :fields] / den

    @pl.loop(1, domains)
    def _(k):
        slot = (dom + k) % domains
        main_copy(k, slot).wait_recv()
        merged_ref[...] += incoming[slot]

    @pl.loop(1, owners)
    def _(k):
        row_copy(k).wait_send()
        stat_copy(k, me).wait_send()

    @pl.loop(1, domains)
    def _(k):
        main_copy(k, dom).wait_send()


def on_device(
    surface_flux,
    active_mask,
    source_area,
    tile_targets,
    remap_tiles,
    ocean_flux,
    air_fraction,
    air_area,
):
    groups = lax.axis_size("comp")
    domains = lax.axis_size("dom")
    owners = groups * domains
    fields = surface_flux.shape[1]
    cells = surface_flux.shape[2]
    blocks, slots, block_cells, air_cells = remap_tiles.shape
    vmem = pl.BlockSpec(memory_space=pltpu.VMEM)
    hbm = pl.BlockSpec(memory_space=pl.ANY)
    dma = pltpu.SemaphoreType.DMA
    return pl.pallas_call(
        functools.partial(kernel, groups, domains),
        out_shape=(
            jax.ShapeDtypeStruct((fields, air_cells), F32),
            jax.ShapeDtypeStruct((groups + 1, fields), F32),
        ),
        in_specs=[hbm, vmem, vmem, vmem, hbm, vmem, vmem, vmem],
        out_specs=(vmem, vmem),
        scratch_shapes=[
            pltpu.VMEM(surface_flux.shape, F32),
            pltpu.VMEM(remap_tiles.shape, F32),
            pltpu.VMEM((16, cells), F32),
            pltpu.VMEM((air_cells // 128, blocks * slots * 16, 128), F32),
            pltpu.VMEM((slots, blocks * slots), jnp.int32),
            pltpu.VMEM((groups, 1, 2 * air_cells), F32),
            pltpu.VMEM((owners, 1, 2 * air_cells), F32),
            pltpu.VMEM((fields, owners, air_cells), F32),
            pltpu.VMEM((fields, domains, air_cells), F32),
            pltpu.VMEM((domains, fields, air_cells), F32),
            pltpu.VMEM((domains, fields, air_cells), F32),
            pltpu.VMEM((16, air_cells), F32),
            pltpu.VMEM((1, 128), F32),
            pltpu.VMEM((owners, 1, 128), F32),
            dma,
            dma((CHUNKS,)),
            dma((owners,)),
            dma((owners,)),
            dma((owners,)),
            dma((owners,)),
            dma,
            dma,
            dma((domains,)),
            dma((domains,)),
        ],
        compiler_params=pltpu.CompilerParams(
            collective_id=0, has_side_effects=True, vmem_limit_bytes=60 * 1024 * 1024
        ),
    )(
        surface_flux,
        active_mask.reshape(1, cells),
        source_area.reshape(1, cells),
        tile_targets.T,
        remap_tiles,
        ocean_flux,
        air_fraction,
        air_area.reshape(1, air_cells),
    )


def solution(mesh):
    in_specs = (
        P(None, None, ("comp", "dom")),
        P(("comp", "dom")),
        P(("comp", "dom")),
        P(("comp", "dom"), None),
        P(("comp", "dom"), None, None, None),
        P(None, ("comp", "dom")),
        P(None, ("comp", "dom")),
        P(("comp", "dom")),
    )
    out_specs = (P(None, ("comp", "dom")), P())
    return jax.shard_map(
        on_device, mesh=mesh, in_specs=in_specs, out_specs=out_specs, check_vma=False
    )
```

time: 82.1 us -> 36.1 us (0.44)
  the two profiles are of different devices: /device:TPU:10 before, /device:TPU:12 now
where the time goes in v1:
time: 36.1 us; the launch traced here: 35.8 us
  Pallas kernels  31.3 us (87%)
  local copies, waits for them, and re-layouts  3.84 us (11%)
  between operations  0.64 us (2%)
    pallas_call x1, Pallas kernels, on_device(): pl.pallas_call(functools.partial(kernel, groups, domains), out_shape=(jax...  31.3 us
    unnamed x2, local copies, waits for them, and re-layouts  2.59 us
    reshape x1, local copies, waits for them, and re-layouts, on_device(): air_area.reshape(1, air_cells)  1.25 us

profile of v1, /device:TPU:12, one launch (start us, length us, event | category | flops | bytes accessed | tf_op | source)
XLA Modules:
  0.0 35.8 jit_solution(16657582103635492227)
XLA Ops:
  0.6 1.2 %reshape.15.air_ref = f32[1,384]{1,0:T(1,128)} reshape(f32[384]{0:T(512)} %param.15) | data formatting | bytes 3072 | tf_op jit(solution)/shard_map/reshape | solution.py:360
  1.9 31.3 %shard_map.95 = (f32[12,384]{1,0:T(8,128)}, f32[3,12]{1,0:T(4,128)}) custom-call(f32[6,12,4096]{2,1,0:T(8,128)} %flux_hbm.1, s32[1,4096]{1,0:T(1,128)} %bitcast.3, f32[1,4096]{1,0:T(1,128)} %bitcast.4, s32[2,64]{1,0:T(2,128)} %bitcast.5, f32[64,2,64,384]{3,2,1,0:T(8,128)} %tiles_hbm.1, f32[12,384]{1,0:T(8,128)} %ocean_ref.1, f32[3,384]{1,0:T(4,128)} %fraction_ref.1, ...), custom_call_target="tpu_custom_call" | custom-call | tf_op jit(solution)/shard_map/pallas_call | solution.py:315
  33.2 1.3 %copy.12 = f32[12,384]{1,0:T(8,128)} copy(f32[12,384]{1,0:T(8,128)} %get-tuple-element.4) | data formatting | bytes 36864
  34.5 1.2 %copy.13 = f32[3,12]{1,0:T(4,128)} copy(f32[3,12]{1,0:T(4,128)} %get-tuple-element.5) | data formatting | bytes 288

commit v2 on v1

--- a/solution.py
+++ b/solution.py
@@ -11,6 +11,8 @@
 F32 = jnp.float32
 BF16 = jnp.bfloat16
 CHUNKS = 8
+DEPTH = 4
+UNROLL = 4
 
 
 def split(x):
@@ -38,18 +40,27 @@
     contrib,
     picks,
     rows_out,
+    rows_own,
     rows_in,
     summed,
     partner_in,
-    outgoing,
-    incoming,
+    outgoing_a,
+    outgoing_b,
+    incoming_a,
+    incoming_b,
     air_rows,
     stat_out,
+    stat_other,
+    stat_sum,
     stat_in,
     flux_sem,
     tile_sem,
+    row_pair_send,
+    row_pair_recv,
     row_send,
     row_recv,
+    stat_pair_send,
+    stat_pair_recv,
     stat_send,
     stat_recv,
     pair_send,
@@ -65,8 +76,9 @@
     tile_count = blocks * slots
     comp = lax.axis_index("comp")
     dom = lax.axis_index("dom")
-    me = comp * domains + dom
     other = 1 - comp
+    outgoing = (outgoing_a, outgoing_b)
+    incoming = (incoming_a, incoming_b)
 
     flux_copy = pltpu.make_async_copy(flux_hbm, flux, flux_sem)
     flux_copy.start()
@@ -74,41 +86,51 @@
     for i in range(CHUNKS):
         part = pl.ds(i * per_chunk, per_chunk)
         copy = pltpu.make_async_copy(tiles_hbm.at[part], tiles.at[part], tile_sem.at[i])
-        copy.start()
+        if i < DEPTH:
+            copy.start()
         tile_copies.append(copy)
 
     barrier = pltpu.get_barrier_semaphore()
 
-    def device(p):
-        return (p // domains, p % domains)
-
-    @pl.loop(1, owners)
-    def _(k):
-        pl.semaphore_signal(
-            barrier, inc=1, device_id=device((me + k) % owners), device_id_type=MESH
-        )
-
+    def peer(k):
+        p = dom + k
+        return jnp.where(p >= domains, p - domains, p)
+
+    peers = list(range(1, domains))
+    pl.semaphore_signal(barrier, inc=1, device_id=(other, dom), device_id_type=MESH)
+    for k in peers:
+        pl.semaphore_signal(barrier, inc=1, device_id=(comp, peer(k)), device_id_type=MESH)
+
+    air = air_ref[...].reshape(1, air_cells)
     for c in range(groups):
         rows_out[c, :, pl.ds(0, air_cells)] = fraction_ref[pl.ds(c, 1), :]
-        rows_out[c, :, pl.ds(air_cells, air_cells)] = air_ref[...]
-    rows_in[me] = rows_out[comp]
-    pl.semaphore_wait(barrier, owners - 1)
-
-    def row_copy(k):
-        p = (me + k) % owners
+        rows_out[c, :, pl.ds(air_cells, air_cells)] = air
+    rows_own[comp] = rows_out[comp]
+
+    row_pair = pltpu.make_async_remote_copy(
+        src_ref=rows_out.at[other],
+        dst_ref=rows_own.at[comp],
+        send_sem=row_pair_send,
+        recv_sem=row_pair_recv,
+        device_id=(other, dom),
+        device_id_type=MESH,
+    )
+
+    def row_copy(k, slot):
         return pltpu.make_async_remote_copy(
-            src_ref=rows_out.at[p // domains],
-            dst_ref=rows_in.at[me],
+            src_ref=rows_own,
+            dst_ref=rows_in.at[:, slot],
             send_sem=row_send.at[k],
-            recv_sem=row_recv.at[me],
-            device_id=device(p),
+            recv_sem=row_recv.at[slot],
+            device_id=(comp, peer(k)),
             device_id_type=MESH,
         )
 
-    @pl.loop(1, owners)
-    def _(k):
-        row_copy(k).start()
-
+    pl.semaphore_wait(barrier, domains)
+    row_pair.start()
+    row_pair.wait()
+    for k in peers:
+        row_copy(k, dom).start()
     flux_copy.wait()
     weighted[pl.ds(8, 8), :] = jnp.zeros((8, cells), F32)
     width = 512
@@ -129,6 +151,7 @@
         cells // width,
         weigh,
         (jnp.zeros((fields, width), F32), jnp.zeros((1, width), F32)),
+        unroll=2,
     )
     surface_num = jnp.sum(total, axis=1, keepdims=True)
     surface_den = jnp.sum(area_total)
@@ -163,7 +186,9 @@
     pairs = per_chunk // 2
     for i in range(CHUNKS):
         tile_copies[i].wait()
-        lax.fori_loop(i * pairs, (i + 1) * pairs, pair, 0)
+        if i + DEPTH < CHUNKS:
+            tile_copies[i + DEPTH].start()
+        lax.fori_loop(i * pairs, (i + 1) * pairs, pair, 0, unroll=UNROLL)
 
     picks[:, pl.ds(0, blocks)] = targets_ref[...]
     picks[:, pl.ds(blocks, blocks)] = targets_ref[...]
@@ -176,23 +201,15 @@
     selector = jnp.where(owner_ids == picked, 1.0, 0.0).astype(BF16)
     selector = jnp.concatenate([selector, selector], axis=1)
 
-    @pl.loop(1, owners)
-    def _(k):
-        p = (me + k) % owners
-        pltpu.make_async_remote_copy(
-            src_ref=rows_out.at[0],
-            dst_ref=rows_in.at[p],
-            send_sem=row_send.at[k],
-            recv_sem=row_recv.at[p],
-            device_id=device(p),
-            device_id_type=MESH,
-        ).wait_recv()
-
-    rows = rows_in[:, 0, :]
+    air_rows[...] = jnp.zeros(air_rows.shape, F32)
+
+    rows_in[:, pl.ds(dom, 1)] = rows_own[...].reshape(groups, 1, 1, 2 * air_cells)
+    for k in peers:
+        row_copy(k, peer(k)).wait_recv()
+
+    rows = rows_in[...].reshape(owners, 2 * air_cells)
     fraction = rows[:, :air_cells]
     scale = fraction / rows[:, air_cells:]
-
-    air_rows[...] = jnp.zeros(air_rows.shape, F32)
 
     def gather(f, carry):
         right = []
@@ -204,21 +221,25 @@
         air_rows[pl.ds(f, 1), :] = jnp.sum(s * fraction, axis=0, keepdims=True)
         return carry
 
-    lax.fori_loop(0, fields, gather, 0)
-
-    pair_copy = pltpu.make_async_remote_copy(
-        src_ref=summed.at[:, pl.ds(pl.multiple_of(other * domains, 8), domains), :],
-        dst_ref=partner_in,
-        send_sem=pair_send,
-        recv_sem=pair_recv,
-        device_id=(other, dom),
-        device_id_type=MESH,
-    )
-    pair_copy.start()
-
+    far = pl.ds(pl.multiple_of(other * domains, 8), domains)
+    cuts = [(0, 8), (8, fields - 8)]
+    pair_copies = []
+    for n, (low, count) in enumerate(cuts):
+        lax.fori_loop(low, low + count, gather, 0, unroll=4)
+        part = pl.ds(low, count)
+        copy = pltpu.make_async_remote_copy(
+            src_ref=summed.at[part, far],
+            dst_ref=partner_in.at[part],
+            send_sem=pair_send.at[n],
+            recv_sem=pair_recv.at[n],
+            device_id=(other, dom),
+            device_id_type=MESH,
+        )
+        copy.start()
+        pair_copies.append(copy)
     ocean = fraction_ref[pl.ds(2, 1), :] * ocean_ref[...]
-    air_num = jnp.sum(air_rows[pl.ds(0, fields), :] + air_ref[...] * ocean, axis=1, keepdims=True)
-    air_den = jnp.sum(air_ref[...])
+    air_num = jnp.sum(air_rows[pl.ds(0, fields), :] + air * ocean, axis=1, keepdims=True)
+    air_den = jnp.sum(air)
     spot = lax.broadcasted_iota(jnp.int32, (fields, 128), 1)
     line = lax.broadcasted_iota(jnp.int32, (fields, 128), 0)
     stat = jnp.where(spot == line + 16 * comp, surface_num, 0.0)
@@ -229,47 +250,69 @@
     stat = stat + jnp.where(spot == dens + comp, surface_den, 0.0)
     stat = stat + jnp.where(spot == dens + groups, air_den, 0.0)
     stat_out[...] = stat
-    stat_in[me] = stat
+    stat_pair = pltpu.make_async_remote_copy(
+        src_ref=stat_out,
+        dst_ref=stat_other,
+        send_sem=stat_pair_send,
+        recv_sem=stat_pair_recv,
+        device_id=(other, dom),
+        device_id_type=MESH,
+    )
+    stat_pair.start()
 
     def stat_copy(k, slot):
         return pltpu.make_async_remote_copy(
-            src_ref=stat_out,
+            src_ref=stat_sum,
             dst_ref=stat_in.at[slot],
             send_sem=stat_send.at[k],
             recv_sem=stat_recv.at[slot],
-            device_id=device((me + k) % owners),
+            device_id=(comp, peer(k)),
             device_id_type=MESH,
         )
 
-    @pl.loop(1, owners)
-    def _(k):
-        stat_copy(k, me).start()
-
-    pair_copy.wait()
     own = pl.ds(pl.multiple_of(comp * domains, 8), domains)
-    for f in range(fields):
-        outgoing[:, f, :] = summed[f, own, :] + partner_in[f]
-
-    def main_copy(k, slot):
-        p = (dom + k) % domains
+
+    def main_copy(n, k, slot):
+        p = peer(k)
         return pltpu.make_async_remote_copy(
-            src_ref=outgoing.at[p],
-            dst_ref=incoming.at[slot],
-            send_sem=main_send.at[k],
-            recv_sem=main_recv.at[slot],
+            src_ref=outgoing[n].at[p],
+            dst_ref=incoming[n].at[slot],
+            send_sem=main_send.at[n, k],
+            recv_sem=main_recv.at[n, slot],
             device_id=(comp, p),
             device_id_type=MESH,
         )
 
-    @pl.loop(1, domains)
-    def _(k):
-        main_copy(k, dom).start()
-
-    merged_ref[...] = ocean + outgoing[dom]
-
-    @pl.loop(1, owners)
-    def _(k):
-        stat_copy(k, (me + k) % owners).wait_recv()
+    def send_group(n):
+        low, count = cuts[n]
+        pair_copies[n].wait()
+        for f in range(low, low + count):
+            outgoing[n][:, f - low, :] = summed[f, own, :] + partner_in[f]
+        for k in peers:
+            main_copy(n, k, dom).start()
+
+    send_group(0)
+    stat_pair.wait()
+    stat = stat_out[...] + stat_other[...]
+    stat_sum[...] = stat
+    stat_in[dom] = stat
+    for k in peers:
+        stat_copy(k, dom).start()
+    send_group(1)
+
+    for n, (low, count) in enumerate(cuts):
+        merged_ref[pl.ds(low, count), :] = ocean[low : low + count] + outgoing[n][dom]
+
+    for n, (low, count) in enumerate(cuts):
+        part = pl.ds(low, count)
+        total = merged_ref[part, :]
+        for k in peers:
+            slot = peer(k)
+            main_copy(n, k, slot).wait_recv()
+            total = total + incoming[n][slot]
+        merged_ref[part, :] = total
+    for k in peers:
+        stat_copy(k, peer(k)).wait_recv()
 
     stat = jnp.sum(stat_in[...], axis=0)
     for c in range(groups + 1):
@@ -277,20 +320,16 @@
         moved = stat if c == 0 else pltpu.roll(stat, 128 - 16 * c, 1)
         means_ref[pl.ds(c, 1), :] = moved[:, :fields] / den
 
-    @pl.loop(1, domains)
-    def _(k):
-        slot = (dom + k) % domains
-        main_copy(k, slot).wait_recv()
-        merged_ref[...] += incoming[slot]
-
-    @pl.loop(1, owners)
-    def _(k):
-        row_copy(k).wait_send()
-        stat_copy(k, me).wait_send()
-
-    @pl.loop(1, domains)
-    def _(k):
-        main_copy(k, dom).wait_send()
+    for k in peers:
+        row_copy(k, dom).wait_send()
+        main_copy(0, k, dom).wait_send()
+        main_copy(1, k, dom).wait_send()
+        stat_copy(k, dom).wait_send()
+
+
+def finish(merged_in, means_in, merged_ref, means_ref):
+    merged_ref[...] = merged_in[...]
+    means_ref[...] = means_in[...]
 
 
 def on_device(
@@ -312,12 +351,13 @@
     vmem = pl.BlockSpec(memory_space=pltpu.VMEM)
     hbm = pl.BlockSpec(memory_space=pl.ANY)
     dma = pltpu.SemaphoreType.DMA
-    return pl.pallas_call(
+    shapes = (
+        jax.ShapeDtypeStruct((fields, air_cells), F32),
+        jax.ShapeDtypeStruct((groups + 1, fields), F32),
+    )
+    parts = pl.pallas_call(
         functools.partial(kernel, groups, domains),
-        out_shape=(
-            jax.ShapeDtypeStruct((fields, air_cells), F32),
-            jax.ShapeDtypeStruct((groups + 1, fields), F32),
-        ),
+        out_shape=shapes,
         in_specs=[hbm, vmem, vmem, vmem, hbm, vmem, vmem, vmem],
         out_specs=(vmem, vmem),
         scratch_shapes=[
@@ -327,24 +367,33 @@
             pltpu.VMEM((air_cells // 128, blocks * slots * 16, 128), F32),
             pltpu.VMEM((slots, blocks * slots), jnp.int32),
             pltpu.VMEM((groups, 1, 2 * air_cells), F32),
-            pltpu.VMEM((owners, 1, 2 * air_cells), F32),
+            pltpu.VMEM((groups, 1, 2 * air_cells), F32),
+            pltpu.VMEM((groups, domains, 1, 2 * air_cells), F32),
             pltpu.VMEM((fields, owners, air_cells), F32),
             pltpu.VMEM((fields, domains, air_cells), F32),
-            pltpu.VMEM((domains, fields, air_cells), F32),
-            pltpu.VMEM((domains, fields, air_cells), F32),
+            pltpu.VMEM((domains, 8, air_cells), F32),
+            pltpu.VMEM((domains, fields - 8, air_cells), F32),
+            pltpu.VMEM((domains, 8, air_cells), F32),
+            pltpu.VMEM((domains, fields - 8, air_cells), F32),
             pltpu.VMEM((16, air_cells), F32),
             pltpu.VMEM((1, 128), F32),
-            pltpu.VMEM((owners, 1, 128), F32),
+            pltpu.VMEM((1, 128), F32),
+            pltpu.VMEM((1, 128), F32),
+            pltpu.VMEM((domains, 1, 128), F32),
             dma,
             dma((CHUNKS,)),
-            dma((owners,)),
-            dma((owners,)),
-            dma((owners,)),
-            dma((owners,)),
             dma,
             dma,
             dma((domains,)),
             dma((domains,)),
+            dma,
+            dma,
+            dma((domains,)),
+            dma((domains,)),
+            dma((2,)),
+            dma((2,)),
+            dma((2, domains)),
+            dma((2, domains)),
         ],
         compiler_params=pltpu.CompilerParams(
             collective_id=0, has_side_effects=True, vmem_limit_bytes=60 * 1024 * 1024
@@ -357,8 +406,11 @@
         remap_tiles,
         ocean_flux,
         air_fraction,
-        air_area.reshape(1, air_cells),
-    )
+        air_area,
+    )
+    return pl.pallas_call(
+        finish, out_shape=shapes, in_specs=[vmem, vmem], out_specs=(vmem, vmem)
+    )(*parts)
 
 
 def solution(mesh):

time: 36.1 us -> 29.6 us (0.82)
  the two profiles are of different devices: /device:TPU:12 before, /device:TPU:0 now
where the time goes in v2:
time: 29.6 us; the launch traced here: 29.3 us
  Pallas kernels  28.7 us (97%)
  between operations  0.64 us (2%)
    pallas_call x1, Pallas kernels, on_device(): pl.pallas_call(functools.partial(kernel, groups, domains), out_shape=shap...  27.3 us
    pallas_call x1, Pallas kernels, on_device(): pl.pallas_call(finish, out_shape=shapes, in_specs=[vmem, vmem], out_specs...  1.35 us

profile of v2, /device:TPU:0, one launch (start us, length us, event | category | flops | bytes accessed | tf_op | source)
XLA Modules:
  0.0 29.3 jit_solution(18445980545590929484)
XLA Ops:
  0.6 27.3 %shard_map.95 = (f32[12,384]{1,0:T(8,128)}, f32[3,12]{1,0:T(4,128)}) custom-call(f32[6,12,4096]{2,1,0:T(8,128)} %flux_hbm.1, s32[1,4096]{1,0:T(1,128)} %bitcast.3, f32[1,4096]{1,0:T(1,128)} %bitcast.4, s32[2,64]{1,0:T(2,128)} %bitcast.5, f32[64,2,64,384]{3,2,1,0:T(8,128)} %tiles_hbm.1, f32[12,384]{1,0:T(8,128)} %ocean_ref.1, f32[3,384]{1,0:T(4,128)} %fraction_ref.1, ...), custom_call_target="tpu_custom_call" | custom-call | tf_op jit(solution)/shard_map/pallas_call | solution.py:358
  28.0 1.4 %shard_map.96 = (f32[12,384]{1,0:T(8,128)}, f32[3,12]{1,0:T(4,128)}) custom-call(f32[12,384]{1,0:T(8,128)} %get-tuple-element.4.merged_in, f32[3,12]{1,0:T(4,128)} %get-tuple-element.5.means_in), custom_call_target="tpu_custom_call" | custom-call | tf_op jit(solution)/shard_map/pallas_call | solution.py:411

commit v3 on v2

--- a/solution.py
+++ b/solution.py
@@ -93,7 +93,7 @@
     barrier = pltpu.get_barrier_semaphore()
 
     def peer(k):
-        p = dom + k
+        p = dom + jnp.where(comp == 0, k, domains - k)
         return jnp.where(p >= domains, p - domains, p)
 
     peers = list(range(1, domains))

time: 29.6 us -> 29.2 us (0.986)
  the two profiles are of different devices: /device:TPU:0 before, /device:TPU:1 now
where the time goes in v3:
time: 29.2 us; the launch traced here: 29 us
  Pallas kernels  28.3 us (97%)
  between operations  0.64 us (2%)
    pallas_call x1, Pallas kernels, on_device(): pl.pallas_call(functools.partial(kernel, groups, domains), out_shape=shap...  27 us
    pallas_call x1, Pallas kernels, on_device(): pl.pallas_call(finish, out_shape=shapes, in_specs=[vmem, vmem], out_specs...  1.35 us

profile of v3, /device:TPU:1, one launch (start us, length us, event | category | flops | bytes accessed | tf_op | source)
XLA Modules:
  0.0 29.0 jit_solution(1000567530031348033)
XLA Ops:
  0.6 27.0 %shard_map.95 = (f32[12,384]{1,0:T(8,128)}, f32[3,12]{1,0:T(4,128)}) custom-call(f32[6,12,4096]{2,1,0:T(8,128)} %flux_hbm.1, s32[1,4096]{1,0:T(1,128)} %bitcast.3, f32[1,4096]{1,0:T(1,128)} %bitcast.4, s32[2,64]{1,0:T(2,128)} %bitcast.5, f32[64,2,64,384]{3,2,1,0:T(8,128)} %tiles_hbm.1, f32[12,384]{1,0:T(8,128)} %ocean_ref.1, f32[3,384]{1,0:T(4,128)} %fraction_ref.1, ...), custom_call_target="tpu_custom_call" | custom-call | tf_op jit(solution)/shard_map/pallas_call | solution.py:358
  27.6 1.4 %shard_map.96 = (f32[12,384]{1,0:T(8,128)}, f32[3,12]{1,0:T(4,128)}) custom-call(f32[12,384]{1,0:T(8,128)} %get-tuple-element.4.merged_in, f32[3,12]{1,0:T(4,128)} %get-tuple-element.5.means_in), custom_call_target="tpu_custom_call" | custom-call | tf_op jit(solution)/shard_map/pallas_call | solution.py:411

commit v4 on v3

--- a/solution.py
+++ b/solution.py
@@ -203,20 +203,27 @@
 
     air_rows[...] = jnp.zeros(air_rows.shape, F32)
 
-    rows_in[:, pl.ds(dom, 1)] = rows_own[...].reshape(groups, 1, 1, 2 * air_cells)
-    for k in peers:
-        row_copy(k, peer(k)).wait_recv()
-
-    rows = rows_in[...].reshape(owners, 2 * air_cells)
-    fraction = rows[:, :air_cells]
-    scale = fraction / rows[:, air_cells:]
-
-    def gather(f, carry):
+    def collect(f, carry):
         right = []
         for q in range(lane_tiles):
             hi, lo = split(contrib[q, pl.ds(f, tile_count, stride=16), :])
             right.append(jnp.concatenate([hi, lo], axis=0))
         s = jnp.dot(selector, jnp.concatenate(right, axis=1), preferred_element_type=F32)
+        summed[f] = s
+        return carry
+
+    lax.fori_loop(0, 8, collect, 0, unroll=4)
+
+    rows_in[:, pl.ds(dom, 1)] = rows_own[...].reshape(groups, 1, 1, 2 * air_cells)
+    for k in peers:
+        row_copy(k, peer(k)).wait_recv()
+
+    rows = rows_in[...].reshape(owners, 2 * air_cells)
+    fraction = rows[:, :air_cells]
+    scale = fraction / rows[:, air_cells:]
+
+    def weigh_sums(f, carry):
+        s = summed[f]
         summed[f] = s * scale
         air_rows[pl.ds(f, 1), :] = jnp.sum(s * fraction, axis=0, keepdims=True)
         return carry
@@ -225,7 +232,9 @@
     cuts = [(0, 8), (8, fields - 8)]
     pair_copies = []
     for n, (low, count) in enumerate(cuts):
-        lax.fori_loop(low, low + count, gather, 0, unroll=4)
+        if n > 0:
+            lax.fori_loop(low, low + count, collect, 0, unroll=4)
+        lax.fori_loop(low, low + count, weigh_sums, 0, unroll=4)
         part = pl.ds(low, count)
         copy = pltpu.make_async_remote_copy(
             src_ref=summed.at[part, far],

time: 29.2 us -> 28.3 us (0.969)
  Pallas kernels: 28.3 us -> 27.4 us
    pallas_call x1, Pallas kernels: 27 us -> 26 us  [on_device(): pl.pallas_call(functools.partial(kernel, groups, domains), out_shape=shap...]
where the time goes in v4:
time: 28.3 us; the launch traced here: 28 us
  Pallas kernels  27.4 us (97%)
  between operations  0.64 us (2%)
    pallas_call x1, Pallas kernels, on_device(): pl.pallas_call(functools.partial(kernel, groups, domains), out_shape=shap...  26 us
    pallas_call x1, Pallas kernels, on_device(): pl.pallas_call(finish, out_shape=shapes, in_specs=[vmem, vmem], out_specs...  1.35 us

profile of v4, /device:TPU:1, one launch (start us, length us, event | category | flops | bytes accessed | tf_op | source)
XLA Modules:
  0.0 28.0 jit_solution(14936957993479926506)
XLA Ops:
  0.6 26.0 %shard_map.95 = (f32[12,384]{1,0:T(8,128)}, f32[3,12]{1,0:T(4,128)}) custom-call(f32[6,12,4096]{2,1,0:T(8,128)} %flux_hbm.1, s32[1,4096]{1,0:T(1,128)} %bitcast.3, f32[1,4096]{1,0:T(1,128)} %bitcast.4, s32[2,64]{1,0:T(2,128)} %bitcast.5, f32[64,2,64,384]{3,2,1,0:T(8,128)} %tiles_hbm.1, f32[12,384]{1,0:T(8,128)} %ocean_ref.1, f32[3,384]{1,0:T(4,128)} %fraction_ref.1, ...), custom_call_target="tpu_custom_call" | custom-call | tf_op jit(solution)/shard_map/pallas_call | solution.py:367
  26.7 1.4 %shard_map.96 = (f32[12,384]{1,0:T(8,128)}, f32[3,12]{1,0:T(4,128)}) custom-call(f32[12,384]{1,0:T(8,128)} %get-tuple-element.4.merged_in, f32[3,12]{1,0:T(4,128)} %get-tuple-element.5.means_in), custom_call_target="tpu_custom_call" | custom-call | tf_op jit(solution)/shard_map/pallas_call | solution.py:420
